TPU v7x, 32 devices: a whole 2x2x4 slice. The times are simulated.
32 devices in a mesh: dp: 8 (over z, y), tensor: 4 (over x, core).
Axes of the slice: x: 2, y: 2, z: 4, core: 2. Of those that a mesh axis runs over, the one named last changes fastest.
Arguments:
- hidden: bfloat16 [2048, 18432], P('dp', 'tensor'), may hold values from -6 to 6
- down_weight: bfloat16 [18432, 4608], P('tensor', 'dp'), may hold values from -0.046875 to 0.046875
- residual: bfloat16 [2048, 4608], P('dp'), may hold values from -6 to 6
- post_gain: float32 [4608], replicated, may hold values from 0.5 to 1.5
- pre_gain: float32 [4608], replicated, may hold values from 0.5 to 1.5
- cast_scale: float32 [1], replicated, may hold values from 100 to 400
- amax_history: float32 [3, 1024], replicated, may hold values from 0.25 to 4
Outputs:
- cast_out: bfloat16 [2048, 4608], P('dp')
- residual_out: bfloat16 [2048, 4608], P('dp')
- peaks: float32 [3], replicated
- new_history: float32 [3, 1024], replicated
- new_scales: float32 [3], replicated
All inputs are finite; a program needn't handle non-finite values.
Results may differ from a plain program's by a relative error of at most 0.012.
Values may be sent and summed in bfloat16 or wider, within the bound.
A program may use at most 128 MiB of HBM per device.

v0:
```python
import jax
import jax.numpy as jnp
from jax import lax
from jax.sharding import PartitionSpec as P

norm_epsilon = 1e-06
float_limit = 448.0


def rms_norm(values, gain_vector):
    return (
        values
        * lax.rsqrt(jnp.mean(values * values, axis=-1, keepdims=True) + norm_epsilon)
        * gain_vector
    )


def finish(summed, stream_in, post_gain, pre_gain, stale_scale):
    stream = stream_in.astype(jnp.float32) + rms_norm(summed, post_gain)
    normed = rms_norm(stream, pre_gain)
    cast_rows = (jnp.clip(normed * stale_scale, -float_limit, float_limit) / stale_scale).astype(
        jnp.bfloat16
    )
    peak_values = jnp.stack(
        [jnp.max(jnp.abs(summed)), jnp.max(jnp.abs(stream)), jnp.max(jnp.abs(normed))]
    )
    return (cast_rows, stream.astype(jnp.bfloat16), peak_values)


def on_device(hidden, down_weight, residual, post_gain, pre_gain, cast_scale, amax_history):
    stale_scale = cast_scale[0]
    partial_value = jnp.dot(
        lax.all_gather(hidden, "dp", axis=0, tiled=True),
        down_weight,
        preferred_element_type=jnp.float32,
    )
    column_total = lax.psum(partial_value.astype(jnp.bfloat16), "tensor").astype(jnp.float32)
    summed = lax.all_to_all(
        column_total.astype(jnp.bfloat16), "dp", split_axis=0, concat_axis=1, tiled=True
    ).astype(column_total.dtype)
    cast_out, residual_out, peak_values = finish(summed, residual, post_gain, pre_gain, stale_scale)
    peak_values = lax.pmax(peak_values, ("dp", "tensor"))
    new_history = jnp.concatenate([peak_values[:, None], amax_history[:, :-1]], axis=1)
    new_scales = float_limit / jnp.maximum(jnp.max(new_history, axis=1), 1.0)
    return (cast_out, residual_out, peak_values, new_history, new_scales)


def solution(mesh):
    in_specs = (P("dp", "tensor"), P("tensor", "dp"), P("dp", None), P(), P(), P(), P())
    out_specs = (P("dp", None), P("dp", None), P(), P(), P())
    return jax.shard_map(
        on_device, mesh=mesh, in_specs=in_specs, out_specs=out_specs, check_vma=False
    )
```

profile of v0, /device:TPU:0, one launch (start us, length us, event | category | flops | bytes accessed | tf_op | source)
XLA Modules:
  0.0 571.7 jit_solution(3271551437250830169)
XLA Ops:
  7.2 0.0 all-gather.2.cloned.1.call-start
  7.2 0.7 all-gather.2.cloned.1.call-update
  7.9 0.0 all-reduce.2.cloned.1.call-start
  7.9 366.7 %all-gather.2.cloned.1.call-done = bf16[2048,4608]{1,0:T(8,128)(2,1)} async-done(((bf16[256,4608]{1,0:T(8,128)(2,1)}), bf16[2048,4608]{1,0:T(8,128)(2,1)}) %all-gather.2.cloned.1.call-update) | async-done | bytes 18874384 | tf_op jit(solution)/shard_map/all_gather | solution.py:33
  374.7 16.5 %convolution_convert_fusion = bf16[2048,576]{0,1:T(8,128)(2,1)S(1)} fusion(bf16[2048,4608]{1,0:T(8,128)(2,1)} %all-gather.2.cloned.1.call-done, bf16[4608,576]{0,1:T(8,128)(2,1)} %param.8), kind=kOutput, calls=%fused_computation.10 | convolution fusion | flops 10872815616 | bytes 26542080 | tf_op jit(solution)/shard_map/dot_general | solution.py:32
  391.2 1.6 copy.21
  392.8 0.0 all-reduce.2.cloned.1.call-update
  392.8 55.8 %all-reduce.2.cloned.1.call-done = bf16[8,256,576]{1,2,0:T(8,128)(2,1)} async-done(((bf16[8,256,576]{1,2,0:T(8,128)(2,1)}), bf16[8,256,576]{1,2,0:T(8,128)(2,1)}) %all-reduce.2.cloned.1.call-update) | async-done | bytes 2359312 | tf_op jit(solution)/shard_map/psum | solution.py:37
  448.6 5.5 all-to-all-start
  454.1 0.0 copy-start.2
  454.1 4.3 copy.14
  458.4 0.0 copy-start.3
  459.0 48.7 %all-to-all-done = bf16[8,256,576]{1,2,0:T(8,128)(2,1)S(1)} async-done(((bf16[8,256,576]{1,2,0:T(8,128)(2,1)}), bf16[8,256,576]{1,2,0:T(8,128)(2,1)S(1)}, u32[]{:S(2)}, u32[]{:S(2)}) %all-to-all-start) | async-done | bytes 2359328 | tf_op jit(solution)/shard_map/all_to_all | solution.py:38
  507.7 0.0 copy-start
  507.7 1.2 abs_reduce_fusion.2
  508.9 0.0 copy-done.2
  508.9 3.3 multiply_reduce_fusion
  512.2 0.0 copy-done.3
  512.2 0.0 copy-done
  512.2 0.0 copy-start.4
  512.2 4.8 abs_reduce_fusion.1
  517.0 0.0 copy-start.1
  517.0 2.2 pad_maximum_fusion.1
  519.2 0.0 copy-done.4
  519.2 0.1 slice_reduce_fusion
  519.3 37.6 %pmax.7 = f32[3]{0:T(128)S(1)} all-reduce(f32[3]{0:T(128)S(1)} %pad_maximum_fusion.1), channel_id=1, replica_groups=mesh['dp'=8,'tensor'=4] {'dp','tensor'}, use_global_device_ids=true, to_apply=%region_6.7 | all-reduce | flops 3 | bytes 24 | tf_op jit(solution)/shard_map/pmax | solution.py:42
  556.9 0.0 copy-start.5
  556.9 0.1 copy.16
  557.0 0.5 maximum_divide_fusion
  557.5 4.3 copy.17
  561.8 0.0 copy-done.1
  561.8 2.4 copy.18
  564.2 0.0 copy-done.5
  564.2 0.7 pad_maximum_fusion
  (2 shorter events, 0.0 us)
Async XLA Ops:
  7.2 367.5 %all-gather.2.cloned.1.call-start = ((), (), s32[]{:S(2)}) async-start(), calls=%async_computation.1 | async-start | bytes 21233664 | tf_op jit(solution)/shard_map/all_gather | solution.py:33
  7.9 440.7 %all-reduce.2.cloned.1.call-start = ((), (), s32[]{:S(2)}) async-start(), calls=%async_computation.2 | async-start | bytes 4718592 | tf_op jit(solution)/shard_map/psum | solution.py:37
  448.6 59.1 %all-to-all-start = ((bf16[8,256,576]{1,2,0:T(8,128)(2,1)}), bf16[8,256,576]{1,2,0:T(8,128)(2,1)S(1)}, u32[]{:S(2)}, u32[]{:S(2)}) async-start(bf16[8,256,576]{1,2,0:T(8,128)(2,1)} %all-reduce.2.cloned.1.call-done), calls=%async_computation | async-start | bytes 4718592 | tf_op jit(solution)/shard_map/all_to_all | solution.py:38
  454.1 54.8 %copy-start.2 = (f32[4608]{0:T(1024)S(1)}, f32[4608]{0:T(1024)}, u32[]{:S(2)}) copy-start(f32[4608]{0:T(1024)} %param.10) | copy-start | bytes 55300
  458.4 53.8 %copy-start.3 = (f32[4608]{0:T(1024)S(1)}, f32[4608]{0:T(1024)}, u32[]{:S(2)}) copy-start(f32[4608]{0:T(1024)} %param.11) | copy-start | bytes 55300
  507.7 4.5 copy-start
  512.2 7.0 %copy-start.4 = (f32[3,1024]{1,0:T(4,128)S(1)}, f32[3,1024]{1,0:T(4,128)}, u32[]{:S(2)}) copy-start(f32[3,1024]{1,0:T(4,128)} %param.13) | copy-start | bytes 36868
  517.0 44.8 %copy-start.1 = (bf16[256,4608]{0,1:T(8,128)(2,1)S(1)}, bf16[256,4608]{0,1:T(8,128)(2,1)}, u32[]{:S(2)}) copy-start(bf16[256,4608]{0,1:T(8,128)(2,1)} %get-tuple-element.15) | copy-start | bytes 7077892
  556.9 7.3 %copy-start.5 = (f32[3]{0:T(128)}, f32[3]{0:T(128)S(1)}, u32[]{:S(2)}) copy-start(f32[3]{0:T(128)S(1)} %pmax.7) | copy-start | bytes 40
Sparse Core Ops, SparseCore 0:
  9.5 365.1 all-gather.1
  392.9 55.5 all-reduce.1
where the time goes:
time: 572 us
  waiting for transfers between devices  472 us (83%)
  blocking collectives  37.6 us (7%)
  matrix products  16.5 us (3%)
  between operations  14.7 us (3%)
  other arithmetic  12.8 us (2%)
  local copies, waits for them, and re-layouts  12.6 us (2%)
    all_gather x1, waiting for transfers between devices, on_device(): lax.all_gather(hidden, 'dp', axis=0, tiled=True)  367 us
    psum x1, waiting for transfers between devices, on_device(): lax.psum(partial_value.astype(jnp.bfloat16), 'tensor').astype(jnp.float32)  55.8 us
    all_to_all x1, waiting for transfers between devices, on_device(): lax.all_to_all(column_total.astype(jnp.bfloat16), 'dp', split_axis=0, con...  48.7 us
    pmax x1, blocking collectives, on_device(): peak_values = lax.pmax(peak_values, ('dp', 'tensor'))  37.6 us
    dot_general x1, matrix products, on_device(): jnp.dot(lax.all_gather(hidden, 'dp', axis=0, tiled=True), down_weight, pr...  16.5 us
  transfers between devices with their start and end apart: 3, of which 3 were waited for; matrix products, arithmetic and copies ran while one was open for 1% of the time, Pallas kernels for 0%

commit v1 on v0

v1 whole, which is shorter than its diff:
```python
import functools

import jax
import jax.numpy as jnp
from jax import lax
from jax.experimental import pallas as pl
from jax.experimental.pallas import tpu as pltpu
from jax.sharding import PartitionSpec as P

MESH = pl.DeviceIdType.MESH
norm_epsilon = 1e-06
float_limit = 448.0
CHUNKS = 2


def rms_norm(values, gain_vector):
    return (
        values
        * lax.rsqrt(jnp.mean(values * values, axis=-1, keepdims=True) + norm_epsilon)
        * gain_vector
    )


def factor(mesh):
    devices = mesh.devices
    count = devices.shape[0]
    coords = [tuple(devices[i, 0].coords) for i in range(count)]
    inner = 1
    if count > 1:
        axis = [p != q for p, q in zip(coords[0], coords[1])].index(True)
        while inner < count and all(
            p == q for k, (p, q) in enumerate(zip(coords[0], coords[inner])) if k != axis
        ):
            inner += 1
    outer = count // inner
    if outer >= inner:
        return (outer, inner), (inner, 1)
    return (inner, 1), (outer, inner)


def project_kernel(dims, hid, wei, out, abuf, wbuf, pbuf, rbuf, sbuf, srec, gbuf,
                   loc_sem, a_send, a_recv, w_send, w_recv, p_send, p_recv,
                   s_send, s_recv, g_send, g_recv):
    (na, sa), (nw, sw), nt, half, rr = dims
    d = lax.axis_index("dp")
    t = lax.axis_index("tensor")
    a = lax.rem(lax.div(d, sa), na)
    w = lax.rem(lax.div(d, sw), nw)

    def dev(a_, w_, t_):
        return (a_ * sa + w_ * sw, t_)

    def copy(src, dst, ss, rs, to):
        return pltpu.make_async_remote_copy(
            src_ref=src, dst_ref=dst, send_sem=ss, recv_sem=rs,
            device_id=to, device_id_type=MESH)

    barrier = pltpu.get_barrier_semaphore()
    for o in range(1, na):
        pl.semaphore_signal(barrier, inc=1, device_id=dev(lax.rem(a + o, na), w, t), device_id_type=MESH)
    for o in range(1, nw):
        pl.semaphore_signal(barrier, inc=1, device_id=dev(a, lax.rem(w + o, nw), t), device_id_type=MESH)
    for o in range(1, nt):
        pl.semaphore_signal(barrier, inc=1, device_id=dev(a, w, lax.rem(t + o, nt)), device_id_type=MESH)
    pl.semaphore_wait(barrier, na + nw + nt - 3)

    def a_copy(src, b, s, dr, h):
        return copy(src, abuf.at[b, h], a_send.at[dr, s, h], a_recv.at[dr, s + 1, h],
                    dev(a - (2 * dr - 1), w, t))

    for h in range(CHUNKS):
        for dr in range(2):
            target = a - (2 * dr - 1)

            @pl.when((target >= 0) & (target < na))
            def _():
                a_copy(hid.at[pl.ds(h * half, half), :], a, 0, dr, h).start()
    for o in range(1, nw):
        p = lax.rem(w + o, nw)
        copy(wei, wbuf.at[w], w_send.at[p], w_recv.at[w], dev(a, p, t)).start()
    locals_ = [pltpu.make_async_copy(wei, wbuf.at[w], loc_sem.at[CHUNKS])]
    locals_ += [
        pltpu.make_async_copy(hid.at[pl.ds(h * half, half), :], abuf.at[a, h], loc_sem.at[h])
        for h in range(CHUNKS)
    ]
    for c in locals_:
        c.start()
    for c in locals_:
        c.wait()

    def mm(b, h, slot):
        term = jnp.dot(abuf[b, h], wbuf[slot], preferred_element_type=jnp.float32)
        term = term.astype(pbuf.dtype)
        for k in range(nt):
            pbuf[b, h, k, slot] = term[k * rr:(k + 1) * rr]

    def p_copy(b, h, peer, me):
        return copy(pbuf.at[b, h, peer], rbuf.at[b, h, me], p_send.at[b, h, peer],
                    p_recv.at[b, h, me], dev(a, w, peer))

    def s_copy(b, h, src):
        return copy(sbuf.at[b, h], srec.at[src, h], s_send.at[b, h], s_recv.at[src, h], dev(b, w, t))

    def g_copy(src, h, peer, me):
        return copy(srec.at[src, h], gbuf.at[src, h, me], g_send.at[src, h, peer],
                    g_recv.at[src, h, me], dev(a, w, peer))

    def send_terms(b, h):
        for o in range(1, nt):
            p_copy(b, h, lax.rem(t + o, nt), t).start()

    def add_terms(b, h):
        total = pbuf[b, h, t].astype(jnp.float32)
        for o in range(1, nt):
            peer = lax.rem(t + o, nt)
            p_copy(b, h, peer, peer).wait_recv()
            total = total + rbuf[b, h, peer].astype(jnp.float32)
        total = total.astype(sbuf.dtype)

        @pl.when(b == a)
        def _():
            srec[b, h] = total

        @pl.when(b != a)
        def _():
            sbuf[b, h] = total
            s_copy(b, h, a).start()

    def spread(src, h):
        @pl.when(src != a)
        def _():
            s_copy(src, h, src).wait_recv()

        for o in range(1, nt):
            g_copy(src, h, lax.rem(t + o, nt), t).start()

    def loop(n, body):
        lax.fori_loop(0, n, lambda i, c: (body(i), c)[1], 0)

    loop(CHUNKS, lambda h: mm(a, h, w))

    def arrive(b, s, dr, h):
        a_copy(abuf.at[b, h], b, s - 1, dr, h).wait_recv()
        target = a - (2 * dr - 1)

        @pl.when((target >= 0) & (target < na))
        def _():
            a_copy(abuf.at[b, h], b, s, dr, h).start()

    def step(i):
        dr = lax.rem(i, 2)
        h = lax.rem(lax.div(i, 2), CHUNKS)
        s = lax.div(i, 2 * CHUNKS) + 1
        b = a + (2 * dr - 1) * s

        @pl.when((b >= 0) & (b < na))
        def _():
            arrive(b, s, dr, h)
            mm(b, h, w)

    loop((na - 2) * 2 * CHUNKS, step)

    for o in range(1, nw):
        p = lax.rem(w + o, nw)
        copy(wei, wbuf.at[p], w_send.at[p], w_recv.at[p], dev(a, p, t)).wait_recv()

    def near(i, body):
        b, h = lax.div(i, CHUNKS), lax.rem(i, CHUNKS)

        @pl.when((b - a <= na - 2) & (a - b <= na - 2))
        def _():
            body(b, h)

    def others(b, h):
        loop(nw - 1, lambda o: mm(b, h, lax.rem(w + 1 + o, nw)))
        send_terms(b, h)

    loop(na * CHUNKS, lambda i: near(i, others))
    loop(na * CHUNKS, lambda i: near(i, add_terms))
    loop(na * CHUNKS, lambda i: near(i, spread))

    @pl.when((a == 0) | (a == na - 1))
    def _():
        far = na - 1 - a
        dr = jnp.where(a == 0, 1, 0)

        def last(h):
            arrive(far, na - 1, dr, h)
            loop(nw, lambda o: mm(far, h, lax.rem(w + o, nw)))
            send_terms(far, h)
            add_terms(far, h)
            spread(far, h)

        loop(CHUNKS, last)

    def collect(i):
        b, h = lax.div(i, CHUNKS), lax.rem(i, CHUNKS)
        for o in range(1, nt):
            peer = lax.rem(t + o, nt)
            g_copy(b, h, peer, peer).wait_recv()
            out[b, h, peer] = gbuf[b, h, peer]
        out[b, h, t] = srec[b, h]

    loop(na * CHUNKS, collect)

    def drain(i):
        b, h = lax.div(i, CHUNKS), lax.rem(i, CHUNKS)
        for o in range(1, nt):
            peer = lax.rem(t + o, nt)
            p_copy(b, h, peer, t).wait_send()
            g_copy(b, h, peer, t).wait_send()

        @pl.when(b != a)
        def _():
            s_copy(b, h, a).wait_send()

    loop(na * CHUNKS, drain)

    def drain_a(i):
        dr = lax.rem(i, 2)
        h = lax.rem(lax.div(i, 2), CHUNKS)
        s = lax.div(i, 2 * CHUNKS)
        b = a + (2 * dr - 1) * s
        target = a - (2 * dr - 1)

        @pl.when((b >= 0) & (b < na) & (target >= 0) & (target < na))
        def _():
            a_copy(abuf.at[b, h], b, s, dr, h).wait_send()

    loop((na - 1) * 2 * CHUNKS, drain_a)
    for o in range(1, nw):
        p = lax.rem(w + o, nw)
        copy(wei, wbuf.at[w], w_send.at[p], w_recv.at[w], dev(a, p, t)).wait_send()


def peak_kernel(n, x, out, got, ss, rs):
    d = lax.axis_index("dp")
    t = lax.axis_index("tensor")
    barrier = pltpu.get_barrier_semaphore()
    for o in range(1, n):
        pl.semaphore_signal(barrier, inc=1, device_id=(lax.rem(d + o, n), t), device_id_type=MESH)
    pl.semaphore_wait(barrier, n - 1)

    def copy(o, slot):
        return pltpu.make_async_remote_copy(
            src_ref=x, dst_ref=got.at[slot], send_sem=ss.at[o], recv_sem=rs.at[slot],
            device_id=(lax.rem(d + o, n), t), device_id_type=MESH)

    for o in range(1, n):
        copy(o, o).start()
    best = x[...]
    for o in range(1, n):
        copy(o, o).wait_recv()
        best = jnp.maximum(best, got[o])
    for o in range(1, n):
        copy(o, o).wait_send()
    out[...] = best


def all_max(values, n):
    return pl.pallas_call(
        functools.partial(peak_kernel, n),
        out_shape=jax.ShapeDtypeStruct(values.shape, values.dtype),
        in_specs=[pl.BlockSpec(memory_space=pltpu.VMEM)],
        out_specs=pl.BlockSpec(memory_space=pltpu.VMEM),
        scratch_shapes=[
            pltpu.VMEM((n,) + values.shape, values.dtype),
            pltpu.SemaphoreType.DMA((n,)),
            pltpu.SemaphoreType.DMA((n,)),
        ],
        compiler_params=pltpu.CompilerParams(collective_id=1, has_side_effects=True),
    )(values)


def project(hidden, down_weight, long, short, nt):
    rows, depth = hidden.shape
    cols = down_weight.shape[1]
    na, nw = long[0], short[0]
    half = rows // CHUNKS
    rr = half // nt
    kind = hidden.dtype
    dma = pltpu.SemaphoreType.DMA
    return pl.pallas_call(
        functools.partial(project_kernel, (long, short, nt, half, rr)),
        out_shape=jax.ShapeDtypeStruct((na, CHUNKS, nt, nw, rr, cols), kind),
        in_specs=[pl.BlockSpec(memory_space=pl.ANY)] * 2,
        out_specs=pl.BlockSpec(memory_space=pltpu.VMEM),
        scratch_shapes=[
            pltpu.VMEM((na, CHUNKS, half, depth), kind),
            pltpu.VMEM((nw, depth, cols), kind),
            pltpu.VMEM((na, CHUNKS, nt, nw, rr, cols), kind),
            pltpu.VMEM((na, CHUNKS, nt, nw, rr, cols), kind),
            pltpu.VMEM((na, CHUNKS, nw, rr, cols), kind),
            pltpu.VMEM((na, CHUNKS, nw, rr, cols), kind),
            pltpu.VMEM((na, CHUNKS, nt, nw, rr, cols), kind),
            dma((CHUNKS + 1,)),
            dma((2, na, CHUNKS)), dma((2, na + 1, CHUNKS)),
            dma((nw,)), dma((nw,)),
            dma((na, CHUNKS, nt)), dma((na, CHUNKS, nt)),
            dma((na, CHUNKS)), dma((na, CHUNKS)),
            dma((na, CHUNKS, nt)), dma((na, CHUNKS, nt)),
        ],
        compiler_params=pltpu.CompilerParams(
            collective_id=0, has_side_effects=True, vmem_limit_bytes=60 * 1024 * 1024),
    )(hidden, down_weight)


def on_device(long, short, nt, hidden, down_weight, residual, post_gain, pre_gain, cast_scale, amax_history):
    stale_scale = cast_scale[0]
    parts = project(hidden, down_weight, long, short, nt)
    order = (1, 2, 4, 0, 3, 5) if long[1] > short[1] else (1, 2, 4, 3, 0, 5)
    summed = parts.transpose(order).reshape(residual.shape).astype(jnp.float32)
    stream = residual.astype(jnp.float32) + rms_norm(summed, post_gain)
    normed = rms_norm(stream, pre_gain)
    cast_out = (jnp.clip(normed * stale_scale, -float_limit, float_limit) / stale_scale).astype(
        jnp.bfloat16
    )
    peak_values = jnp.stack(
        [jnp.max(jnp.abs(summed)), jnp.max(jnp.abs(stream)), jnp.max(jnp.abs(normed))]
    )
    tile = jnp.zeros((8, 128), jnp.float32).at[:3, :].set(peak_values[:, None])
    peak_values = all_max(tile, long[0] * short[0])[:3, 0]
    new_history = jnp.concatenate([peak_values[:, None], amax_history[:, :-1]], axis=1)
    new_scales = float_limit / jnp.maximum(jnp.max(new_history, axis=1), 1.0)
    return (cast_out, stream.astype(jnp.bfloat16), peak_values, new_history, new_scales)


def solution(mesh):
    long, short = factor(mesh)
    in_specs = (P("dp", "tensor"), P("tensor", "dp"), P("dp", None), P(), P(), P(), P())
    out_specs = (P("dp", None), P("dp", None), P(), P(), P())
    return jax.shard_map(
        functools.partial(on_device, long, short, mesh.shape["tensor"]),
        mesh=mesh, in_specs=in_specs, out_specs=out_specs, check_vma=False
    )
```

time: 572 us -> 265 us (0.46)
  waiting for transfers between devices: 472 us -> 0 us
  Pallas kernels: 0 us -> 221 us
  blocking collectives: 37.6 us -> 0 us
  matrix products: 16.5 us -> 0 us
  between operations: 14.7 us -> 1.35 us
  local copies, waits for them, and re-layouts: 12.6 us -> 24.7 us
    all_gather x1 -> x0, waiting for transfers between devices: 367 us -> none  [on_device(): lax.all_gather(hidden, 'dp', axis=0, tiled=True)]
    pallas_call x0 -> x2, Pallas kernels: none -> 221 us  [the longest x1 211 us: project(): pl.pallas_call(functools.partial(project_kernel, (long, short, nt, half,...]
    psum x1 -> x0, waiting for transfers between devices: 55.8 us -> none  [on_device(): lax.psum(partial_value.astype(jnp.bfloat16), 'tensor').astype(jnp.float32)]
    all_to_all x1 -> x0, waiting for transfers between devices: 48.7 us -> none  [on_device(): lax.all_to_all(column_total.astype(jnp.bfloat16), 'dp', split_axis=0, con...]
    pmax x1 -> x0, blocking collectives: 37.6 us -> none  [on_device(): peak_values = lax.pmax(peak_values, ('dp', 'tensor'))]
    dot_general x1 -> x0, matrix products: 16.5 us -> none  [on_device(): jnp.dot(lax.all_gather(hidden, 'dp', axis=0, tiled=True), down_weight, pr...]
    convert_element_type x0 -> x2, local copies, waits for them, and re-layouts: none -> 14.7 us  [on_device(): summed = parts.transpose(order).reshape(residual.shape).astype(jnp.float32)]
    convert_element_type x0 -> x2, other arithmetic: none -> 7.15 us  [the longest x1 4.72 us: on_device(): stream.astype(jnp.bfloat16)]
  transfers between devices with their start and end apart: 3 -> 0, of which waited for: 3 -> 0; matrix products, arithmetic and copies ran while one was open for 1% -> 0% of each run, Pallas kernels for 0% -> 0%
where the time goes in v1:
time: 265 us; the launch traced here: 264 us
  Pallas kernels  221 us (83%)
  local copies, waits for them, and re-layouts  24.7 us (9%)
  other arithmetic  17.3 us (7%)
    pallas_call x1, Pallas kernels, project(): pl.pallas_call(functools.partial(project_kernel, (long, short, nt, half,...  211 us
    convert_element_type x2, local copies, waits for them, and re-layouts, on_device(): summed = parts.transpose(order).reshape(residual.shape).astype(jnp.float32)  14.7 us
    pallas_call x1, Pallas kernels, all_max(): pl.pallas_call(functools.partial(peak_kernel, n), out_shape=jax.ShapeDtyp...  9.75 us
    unnamed x11, local copies, waits for them, and re-layouts  8.41 us

profile of v1, /device:TPU:0, one launch (start us, length us, event | category | flops | bytes accessed | tf_op | source)
XLA Modules:
  0.0 263.9 jit_solution(8255921629339743248)
XLA Ops:
  0.6 8.4 %copy.13.wei = bf16[4608,576]{1,0:T(8,128)(2,1)} copy(bf16[4608,576]{0,1:T(8,128)(2,1)} %param.10) | data formatting | bytes 10616832 | tf_op args[1]
  9.0 210.9 %shard_map.110 = bf16[4,2,4,2,32,576]{5,4,3,2,1,0:T(8,128)(2,1)} custom-call(bf16[256,4608]{1,0:T(8,128)(2,1)} %hid.1, bf16[4608,576]{1,0:T(8,128)(2,1)} %copy.13.wei), custom_call_target="tpu_custom_call" | custom-call | tf_op jit(solution)/shard_map/pallas_call | solution.py:283
  220.0 3.1 %fusion.1 = (f32[]{:T(128)}, f32[2,4,32]{2,1,0:T(4,128)S(1)}) fusion(bf16[4,2,4,2,32,576]{5,4,3,2,1,0:T(8,128)(2,1)} %shard_map.110), kind=kLoop, calls=%fused_computation.4 | loop fusion | flops 5897983 | bytes 2360324 | tf_op jit(solution)/shard_map/reduce_max | solution.py:319
  223.1 0.1 rsqrt.20
  223.2 2.4 convert_bitcast_fusion
  225.6 6.4 %copy.14 = f32[2,4,32,4,2,576]{5,4,3,2,1,0:T(2,128)} copy(f32[2,4,32,4,2,576]{5,2,4,1,0,3:T(8,128)S(1)} %convert_bitcast_fusion) | data formatting | bytes 9437184 | tf_op jit(solution)/shard_map/convert_element_type | solution.py:312
  232.0 0.0 copy-start
  232.0 0.0 copy-start.1
  232.0 8.3 %reshape.66 = f32[256,4608]{1,0:T(8,128)} reshape(f32[2,4,32,4,2,576]{5,4,3,2,1,0:T(2,128)} %copy.14) | data formatting | bytes 9437184 | tf_op jit(solution)/shard_map/convert_element_type | solution.py:312
  240.3 0.0 copy-done
  240.3 0.0 copy-done.1
  240.3 4.7 %fusion.2 = (bf16[256,4608]{1,0:T(8,128)(2,1)}, f32[256,4608]{1,0:T(8,128)S(1)}) fusion(f32[4608]{0:T(1024)S(1)} %copy-done.1, f32[256,4608]{1,0:T(8,128)} %reshape.66, f32[256]{0:T(256)S(1)} %rsqrt.20, bf16[256,4608]{1,0:T(8,128)(2,1)S(1)} %copy-done), kind=kLoop, calls=%fused_computation.20 | loop fusion | flops 5898240 | bytes 14175232 | tf_op jit(solution)/shard_map/convert_element_type | solution.py:325
  245.0 0.0 copy-start.2
  245.1 0.4 multiply_reduce_fusion
  245.5 0.0 copy-start.3
  246.1 0.0 copy-done.2
  246.1 3.2 %abs_reduce_fusion.1 = (f32[]{:T(128)}, f32[]{:T(128)}, bf16[256,4608]{1,0:T(8,128)(2,1)}) fusion(f32[256,4608]{1,0:T(8,128)S(1)} %get-tuple-element.22, f32[4608]{0:T(1024)S(1)} %copy-done.2, f32[256]{0:T(256)S(1)} %add_rsqrt_fusion.1, f32[]{:T(128)} %bitcast.6), kind=kLoop, calls=%fused_computation.6 | loop fusion | flops 11796478 | bytes 7097356 | tf_op jit(solution)/shard_map/reduce_max | solution.py:319
  249.3 2.1 select_maximum_fusion
  251.4 0.7 scatter.8.x
  252.0 9.7 %shard_map.111 = f32[8,128]{1,0:T(8,128)} custom-call(f32[8,128]{1,0:T(8,128)} %scatter.8.x), custom_call_target="tpu_custom_call" | custom-call | tf_op jit(solution)/shard_map/pallas_call | solution.py:261
  261.8 0.8 fusion.3
  262.6 0.0 copy-start.4
  262.6 0.0 copy-done.3
  262.6 0.1 slice_reduce_fusion.1
  262.7 0.5 maximum_divide_fusion
  263.3 0.7 pad_maximum_fusion
  263.9 0.0 copy-done.4
  (2 shorter events, 0.0 us)
Async XLA Ops:
  232.0 8.3 %copy-start = (bf16[256,4608]{1,0:T(8,128)(2,1)S(1)}, bf16[256,4608]{1,0:T(8,128)(2,1)}, u32[]{:S(2)}) copy-start(bf16[256,4608]{1,0:T(8,128)(2,1)} %param.11) | copy-start | bytes 7077892
  232.0 8.3 %copy-start.1 = (f32[4608]{0:T(1024)S(1)}, f32[4608]{0:T(1024)}, u32[]{:S(2)}) copy-start(f32[4608]{0:T(1024)} %param.12) | copy-start | bytes 55300
  245.0 1.1 copy-start.2
  245.5 17.1 %copy-start.3 = (f32[3,1024]{1,0:T(4,128)S(1)}, f32[3,1024]{1,0:T(4,128)}, u32[]{:S(2)}) copy-start(f32[3,1024]{1,0:T(4,128)} %param.15) | copy-start | bytes 36868
  262.6 1.3 copy-start.4

commit v2 on v1

--- a/solution.py
+++ b/solution.py
@@ -89,55 +89,62 @@
         c.wait()
 
     def mm(b, h, slot):
-        term = jnp.dot(abuf[b, h], wbuf[slot], preferred_element_type=jnp.float32)
+        term = lax.dot_general(
+            abuf[b, h], wbuf[slot], (((1,), (1,)), ((), ())),
+            preferred_element_type=jnp.float32)
         term = term.astype(pbuf.dtype)
         for k in range(nt):
             pbuf[b, h, k, slot] = term[k * rr:(k + 1) * rr]
 
-    def p_copy(b, h, peer, me):
-        return copy(pbuf.at[b, h, peer], rbuf.at[b, h, me], p_send.at[b, h, peer],
-                    p_recv.at[b, h, me], dev(a, w, peer))
-
-    def s_copy(b, h, src):
-        return copy(sbuf.at[b, h], srec.at[src, h], s_send.at[b, h], s_recv.at[src, h], dev(b, w, t))
-
-    def g_copy(src, h, peer, me):
-        return copy(srec.at[src, h], gbuf.at[src, h, me], g_send.at[src, h, peer],
-                    g_recv.at[src, h, me], dev(a, w, peer))
-
-    def send_terms(b, h):
+    def p_copy(b, h, slot, peer, me):
+        return copy(pbuf.at[b, h, peer, slot], rbuf.at[b, h, me, slot],
+                    p_send.at[b, h, peer, slot], p_recv.at[b, h, me, slot], dev(a, w, peer))
+
+    def s_copy(b, h, slot, src):
+        return copy(sbuf.at[b, h, slot], srec.at[src, h, slot], s_send.at[b, h, slot],
+                    s_recv.at[src, h, slot], dev(b, w, t))
+
+    def g_copy(src, h, slot, peer, me):
+        return copy(srec.at[src, h, slot], gbuf.at[src, h, me, slot],
+                    g_send.at[src, h, peer, slot], g_recv.at[src, h, me, slot], dev(a, w, peer))
+
+    def send_terms(b, h, slot):
         for o in range(1, nt):
-            p_copy(b, h, lax.rem(t + o, nt), t).start()
-
-    def add_terms(b, h):
-        total = pbuf[b, h, t].astype(jnp.float32)
+            p_copy(b, h, slot, lax.rem(t + o, nt), t).start()
+
+    def add_terms(b, h, slot):
+        total = pbuf[b, h, t, slot].astype(jnp.float32)
         for o in range(1, nt):
             peer = lax.rem(t + o, nt)
-            p_copy(b, h, peer, peer).wait_recv()
-            total = total + rbuf[b, h, peer].astype(jnp.float32)
+            p_copy(b, h, slot, peer, peer).wait_recv()
+            total = total + rbuf[b, h, peer, slot].astype(jnp.float32)
         total = total.astype(sbuf.dtype)
 
         @pl.when(b == a)
         def _():
-            srec[b, h] = total
+            srec[b, h, slot] = total
 
         @pl.when(b != a)
         def _():
-            sbuf[b, h] = total
-            s_copy(b, h, a).start()
-
-    def spread(src, h):
+            sbuf[b, h, slot] = total
+            s_copy(b, h, slot, a).start()
+
+    def spread(src, h, slot):
         @pl.when(src != a)
         def _():
-            s_copy(src, h, src).wait_recv()
+            s_copy(src, h, slot, src).wait_recv()
 
         for o in range(1, nt):
-            g_copy(src, h, lax.rem(t + o, nt), t).start()
+            g_copy(src, h, slot, lax.rem(t + o, nt), t).start()
 
     def loop(n, body):
         lax.fori_loop(0, n, lambda i, c: (body(i), c)[1], 0)
 
-    loop(CHUNKS, lambda h: mm(a, h, w))
+    def own(h):
+        mm(a, h, w)
+        send_terms(a, h, w)
+
+    loop(CHUNKS, own)
 
     def arrive(b, s, dr, h):
         a_copy(abuf.at[b, h], b, s - 1, dr, h).wait_recv()
@@ -157,27 +164,34 @@
         def _():
             arrive(b, s, dr, h)
             mm(b, h, w)
+            send_terms(b, h, w)
 
     loop((na - 2) * 2 * CHUNKS, step)
+
+    def near(i, body):
+        b, h = lax.div(i, CHUNKS), lax.rem(i, CHUNKS)
+
+        @pl.when((b - a <= na - 2) & (a - b <= na - 2))
+        def _():
+            body(b, h)
+
+    loop(na * CHUNKS, lambda i: near(i, lambda b, h: add_terms(b, h, w)))
+    loop(na * CHUNKS, lambda i: near(i, lambda b, h: spread(b, h, w)))
 
     for o in range(1, nw):
         p = lax.rem(w + o, nw)
         copy(wei, wbuf.at[p], w_send.at[p], w_recv.at[p], dev(a, p, t)).wait_recv()
 
-    def near(i, body):
-        b, h = lax.div(i, CHUNKS), lax.rem(i, CHUNKS)
-
-        @pl.when((b - a <= na - 2) & (a - b <= na - 2))
-        def _():
-            body(b, h)
-
-    def others(b, h):
-        loop(nw - 1, lambda o: mm(b, h, lax.rem(w + 1 + o, nw)))
-        send_terms(b, h)
-
-    loop(na * CHUNKS, lambda i: near(i, others))
-    loop(na * CHUNKS, lambda i: near(i, add_terms))
-    loop(na * CHUNKS, lambda i: near(i, spread))
+    def each_other(body):
+        return lambda b, h: loop(nw - 1, lambda o: body(b, h, lax.rem(w + 1 + o, nw)))
+
+    def multiply(b, h, slot):
+        mm(b, h, slot)
+        send_terms(b, h, slot)
+
+    loop(na * CHUNKS, lambda i: near(i, each_other(multiply)))
+    loop(na * CHUNKS, lambda i: near(i, each_other(add_terms)))
+    loop(na * CHUNKS, lambda i: near(i, each_other(spread)))
 
     @pl.when((a == 0) | (a == na - 1))
     def _():
@@ -186,10 +200,9 @@
 
         def last(h):
             arrive(far, na - 1, dr, h)
-            loop(nw, lambda o: mm(far, h, lax.rem(w + o, nw)))
-            send_terms(far, h)
-            add_terms(far, h)
-            spread(far, h)
+            loop(nw, lambda slot: multiply(far, h, slot))
+            loop(nw, lambda slot: add_terms(far, h, slot))
+            loop(nw, lambda slot: spread(far, h, slot))
 
         loop(CHUNKS, last)
 
@@ -197,7 +210,8 @@
         b, h = lax.div(i, CHUNKS), lax.rem(i, CHUNKS)
         for o in range(1, nt):
             peer = lax.rem(t + o, nt)
-            g_copy(b, h, peer, peer).wait_recv()
+            for slot in range(nw):
+                g_copy(b, h, slot, peer, peer).wait_recv()
             out[b, h, peer] = gbuf[b, h, peer]
         out[b, h, t] = srec[b, h]
 
@@ -205,14 +219,15 @@
 
     def drain(i):
         b, h = lax.div(i, CHUNKS), lax.rem(i, CHUNKS)
-        for o in range(1, nt):
-            peer = lax.rem(t + o, nt)
-            p_copy(b, h, peer, t).wait_send()
-            g_copy(b, h, peer, t).wait_send()
-
-        @pl.when(b != a)
-        def _():
-            s_copy(b, h, a).wait_send()
+        for slot in range(nw):
+            for o in range(1, nt):
+                peer = lax.rem(t + o, nt)
+                p_copy(b, h, slot, peer, t).wait_send()
+                g_copy(b, h, slot, peer, t).wait_send()
+
+            @pl.when(b != a)
+            def _():
+                s_copy(b, h, slot, a).wait_send()
 
     loop(na * CHUNKS, drain)
 
@@ -233,7 +248,7 @@
         copy(wei, wbuf.at[w], w_send.at[p], w_recv.at[w], dev(a, p, t)).wait_send()
 
 
-def peak_kernel(n, x, out, got, ss, rs):
+def peak_kernel(n, x, hist, peaks, history, scales, got, ss, rs):
     d = lax.axis_index("dp")
     t = lax.axis_index("tensor")
     barrier = pltpu.get_barrier_semaphore()
@@ -252,29 +267,83 @@
     for o in range(1, n):
         copy(o, o).wait_recv()
         best = jnp.maximum(best, got[o])
+    best = best[:3, :1]
+    kept = hist[...]
+    lane = lax.broadcasted_iota(jnp.int32, kept.shape, 1)
+    new = jnp.where(lane == 0, best, pltpu.roll(kept, 1, 1))
+    peaks[...] = best
+    history[...] = new
+    scales[...] = float_limit / jnp.maximum(jnp.max(new, axis=1, keepdims=True), 1.0)
     for o in range(1, n):
         copy(o, o).wait_send()
-    out[...] = best
-
-
-def all_max(values, n):
+
+
+def all_max(values, hist, n):
+    vmem = pl.BlockSpec(memory_space=pltpu.VMEM)
+    column = jax.ShapeDtypeStruct((hist.shape[0], 1), jnp.float32)
     return pl.pallas_call(
         functools.partial(peak_kernel, n),
-        out_shape=jax.ShapeDtypeStruct(values.shape, values.dtype),
-        in_specs=[pl.BlockSpec(memory_space=pltpu.VMEM)],
-        out_specs=pl.BlockSpec(memory_space=pltpu.VMEM),
+        out_shape=(column, jax.ShapeDtypeStruct(hist.shape, hist.dtype), column),
+        in_specs=[vmem] * 2,
+        out_specs=[vmem] * 3,
         scratch_shapes=[
             pltpu.VMEM((n,) + values.shape, values.dtype),
             pltpu.SemaphoreType.DMA((n,)),
             pltpu.SemaphoreType.DMA((n,)),
         ],
         compiler_params=pltpu.CompilerParams(collective_id=1, has_side_effects=True),
-    )(values)
+    )(values, hist)
+
+
+def finish_kernel(dims, scale, parts, residual, post_gain, pre_gain, cast_out, stream_out, peaks, summed):
+    (na, sa), (nw, sw), cols = dims
+    for a in range(na):
+        for w in range(nw):
+            first = (a * sa + w * sw) * cols
+            summed[:, first:first + cols] = parts[a, 0, 0, w].astype(jnp.float32)
+    x = summed[...]
+    stream = residual[...].astype(jnp.float32) + rms_norm(x, post_gain[...])
+    normed = rms_norm(stream, pre_gain[...])
+    s = scale[0]
+    cast_out[...] = (jnp.clip(normed * s, -float_limit, float_limit) / s).astype(cast_out.dtype)
+    stream_out[...] = stream.astype(stream_out.dtype)
+    row = lax.broadcasted_iota(jnp.int32, peaks.shape, 0)
+    tops = [jnp.max(jnp.abs(v)) for v in (x, stream, normed)]
+    tile = jnp.where(row == 0, tops[0], jnp.where(row == 1, tops[1], tops[2]))
+    first_step = (pl.program_id(0) == 0) & (pl.program_id(1) == 0)
+
+    @pl.when(first_step)
+    def _():
+        peaks[...] = tile
+
+    @pl.when(jnp.logical_not(first_step))
+    def _():
+        peaks[...] = jnp.maximum(peaks[...], tile)
+
+
+def finish(parts, residual, post_gain, pre_gain, cast_scale, long, short):
+    na, chunks, nt, nw, rr, cols = parts.shape
+    width = residual.shape[1]
+    rows = pl.BlockSpec((rr, width), lambda h, k: (h * nt + k, 0))
+    gain = pl.BlockSpec((1, width), lambda h, k: (0, 0))
+    kind = jax.ShapeDtypeStruct(residual.shape, jnp.bfloat16)
+    return pl.pallas_call(
+        functools.partial(finish_kernel, (long, short, cols)),
+        grid=(chunks, nt),
+        out_shape=(kind, kind, jax.ShapeDtypeStruct((8, 128), jnp.float32)),
+        in_specs=[
+            pl.BlockSpec(memory_space=pltpu.SMEM),
+            pl.BlockSpec((na, 1, 1, nw, rr, cols), lambda h, k: (0, h, k, 0, 0, 0)),
+            rows, gain, gain,
+        ],
+        out_specs=[rows, rows, pl.BlockSpec((8, 128), lambda h, k: (0, 0))],
+        scratch_shapes=[pltpu.VMEM((rr, width), jnp.float32)],
+    )(cast_scale, parts, residual, post_gain[None], pre_gain[None])
 
 
 def project(hidden, down_weight, long, short, nt):
     rows, depth = hidden.shape
-    cols = down_weight.shape[1]
+    cols = down_weight.shape[0]
     na, nw = long[0], short[0]
     half = rows // CHUNKS
     rr = half // nt
@@ -287,7 +356,7 @@
         out_specs=pl.BlockSpec(memory_space=pltpu.VMEM),
         scratch_shapes=[
             pltpu.VMEM((na, CHUNKS, half, depth), kind),
-            pltpu.VMEM((nw, depth, cols), kind),
+            pltpu.VMEM((nw, cols, depth), kind),
             pltpu.VMEM((na, CHUNKS, nt, nw, rr, cols), kind),
             pltpu.VMEM((na, CHUNKS, nt, nw, rr, cols), kind),
             pltpu.VMEM((na, CHUNKS, nw, rr, cols), kind),
@@ -296,9 +365,9 @@
             dma((CHUNKS + 1,)),
             dma((2, na, CHUNKS)), dma((2, na + 1, CHUNKS)),
             dma((nw,)), dma((nw,)),
-            dma((na, CHUNKS, nt)), dma((na, CHUNKS, nt)),
-            dma((na, CHUNKS)), dma((na, CHUNKS)),
-            dma((na, CHUNKS, nt)), dma((na, CHUNKS, nt)),
+            dma((na, CHUNKS, nt, nw)), dma((na, CHUNKS, nt, nw)),
+            dma((na, CHUNKS, nw)), dma((na, CHUNKS, nw)),
+            dma((na, CHUNKS, nt, nw)), dma((na, CHUNKS, nt, nw)),
         ],
         compiler_params=pltpu.CompilerParams(
             collective_id=0, has_side_effects=True, vmem_limit_bytes=60 * 1024 * 1024),
@@ -306,23 +375,10 @@
 
 
 def on_device(long, short, nt, hidden, down_weight, residual, post_gain, pre_gain, cast_scale, amax_history):
-    stale_scale = cast_scale[0]
-    parts = project(hidden, down_weight, long, short, nt)
-    order = (1, 2, 4, 0, 3, 5) if long[1] > short[1] else (1, 2, 4, 3, 0, 5)
-    summed = parts.transpose(order).reshape(residual.shape).astype(jnp.float32)
-    stream = residual.astype(jnp.float32) + rms_norm(summed, post_gain)
-    normed = rms_norm(stream, pre_gain)
-    cast_out = (jnp.clip(normed * stale_scale, -float_limit, float_limit) / stale_scale).astype(
-        jnp.bfloat16
-    )
-    peak_values = jnp.stack(
-        [jnp.max(jnp.abs(summed)), jnp.max(jnp.abs(stream)), jnp.max(jnp.abs(normed))]
-    )
-    tile = jnp.zeros((8, 128), jnp.float32).at[:3, :].set(peak_values[:, None])
-    peak_values = all_max(tile, long[0] * short[0])[:3, 0]
-    new_history = jnp.concatenate([peak_values[:, None], amax_history[:, :-1]], axis=1)
-    new_scales = float_limit / jnp.maximum(jnp.max(new_history, axis=1), 1.0)
-    return (cast_out, stream.astype(jnp.bfloat16), peak_values, new_history, new_scales)
+    parts = project(hidden, down_weight.T, long, short, nt)
+    cast_out, stream, tile = finish(parts, residual, post_gain, pre_gain, cast_scale, long, short)
+    peaks, new_history, new_scales = all_max(tile, amax_history, long[0] * short[0])
+    return (cast_out, stream, peaks[:, 0], new_history, new_scales[:, 0])
 
 
 def solution(mesh):

time: 265 us -> 245 us (0.925)
  local copies, waits for them, and re-layouts: 24.7 us -> 4.01 us
  Pallas kernels: 221 us -> 237 us
  other arithmetic: 17.3 us -> 2.58 us
    convert_element_type x2 -> x0, local copies, waits for them, and re-layouts: 14.7 us -> none  [on_device(): summed = parts.transpose(order).reshape(residual.shape).astype(jnp.float32)]
    pallas_call x1, Pallas kernels: 211 us -> 219 us  [project(): pl.pallas_call(functools.partial(project_kernel, (long, short, nt, half,...]
    pallas_call x1 -> x2, Pallas kernels: 9.75 us -> 17.4 us  [the longest x1 9.35 us: finish(): pl.pallas_call(functools.partial(finish_kernel, (long, short, cols)), gri...]
    convert_element_type x2 -> x0, other arithmetic: 7.15 us -> none  [the longest x1 4.72 us: on_device(): stream.astype(jnp.bfloat16)]
    unnamed x11 -> x1, local copies, waits for them, and re-layouts: 8.41 us -> 1.32 us
    reduce_max x3 -> x0, other arithmetic: 6.44 us -> none  [the longest x1 3.18 us: on_device(): jnp.max(jnp.abs(stream))]
    broadcast_in_dim x0 -> x2, local copies, waits for them, and re-layouts: none -> 2.68 us  [the longest x1 1.34 us: finish(): post_gain[None]]
where the time goes in v2:
time: 245 us
  Pallas kernels  237 us (97%)
  local copies, waits for them, and re-layouts  4.01 us (2%)
  other arithmetic  2.58 us (1%)
    pallas_call x1, Pallas kernels, project(): pl.pallas_call(functools.partial(project_kernel, (long, short, nt, half,...  219 us
    pallas_call x1, Pallas kernels, finish(): pl.pallas_call(functools.partial(finish_kernel, (long, short, cols)), gri...  9.35 us
    pallas_call x1, Pallas kernels, all_max(): pl.pallas_call(functools.partial(peak_kernel, n), out_shape=(column, jax....  8.01 us

profile of v2, /device:TPU:0, one launch (start us, length us, event | category | flops | bytes accessed | tf_op | source)
XLA Modules:
  0.0 244.7 jit_solution(4785338175925442341)
XLA Ops:
  1.3 1.3 broadcast_in_dim.6.post_gain
  2.6 1.3 broadcast_in_dim.7.pre_gain
  4.0 219.5 %shard_map.110.parts = bf16[4,2,4,2,32,576]{5,4,3,2,1,0:T(8,128)(2,1)} custom-call(bf16[256,4608]{1,0:T(8,128)(2,1)} %hid.1, bf16[576,4608]{1,0:T(8,128)(2,1)} %bitcast.1), custom_call_target="tpu_custom_call" | custom-call | tf_op jit(solution)/shard_map/pallas_call | solution.py:352
  223.5 9.3 %shard_map.111 = (bf16[256,4608]{1,0:T(8,128)(2,1)}, bf16[256,4608]{1,0:T(8,128)(2,1)}, f32[8,128]{1,0:T(8,128)}) custom-call(f32[1]{0:T(128)S(6)} %copy.13.scale, bf16[4,2,4,2,32,576]{5,4,3,2,1,0:T(8,128)(2,1)} %shard_map.110.parts, bf16[256,4608]{1,0:T(8,128)(2,1)} %residual.1, f32[1,4608]{1,0:T(1,128)} %broadcast_in_dim.6.post_gain, ...), custom_call_target="tpu_custom_call" | custom-call | tf_op jit(solution)/shard_map/pallas_call | solution.py:330
  232.8 8.0 %shard_map.112 = (f32[3,1]{1,0:T(4,128)}, f32[3,1024]{1,0:T(4,128)}, f32[3,1]{1,0:T(4,128)}) custom-call(f32[8,128]{1,0:T(8,128)} %get-tuple-element.13.x, f32[3,1024]{1,0:T(4,128)} %hist.1), custom_call_target="tpu_custom_call" | custom-call | tf_op jit(solution)/shard_map/pallas_call | solution.py:284
  240.8 1.3 reduce
  242.1 1.3 reduce.1
  243.4 1.3 copy.14

commit v3 on v2

--- a/solution.py
+++ b/solution.py
@@ -96,6 +96,16 @@
         for k in range(nt):
             pbuf[b, h, k, slot] = term[k * rr:(k + 1) * rr]
 
+    def mm_whole(b, slot):
+        rows = abuf[b].reshape(CHUNKS * half, abuf.shape[-1])
+        term = lax.dot_general(
+            rows, wbuf[slot], (((1,), (1,)), ((), ())), preferred_element_type=jnp.float32)
+        term = term.astype(pbuf.dtype)
+        for h in range(CHUNKS):
+            for k in range(nt):
+                first = h * half + k * rr
+                pbuf[b, h, k, slot] = term[first:first + rr]
+
     def p_copy(b, h, slot, peer, me):
         return copy(pbuf.at[b, h, peer, slot], rbuf.at[b, h, me, slot],
                     p_send.at[b, h, peer, slot], p_recv.at[b, h, me, slot], dev(a, w, peer))
@@ -143,6 +153,7 @@
     def own(h):
         mm(a, h, w)
         send_terms(a, h, w)
+        add_terms(a, h, w)
 
     loop(CHUNKS, own)
 
@@ -165,6 +176,7 @@
             arrive(b, s, dr, h)
             mm(b, h, w)
             send_terms(b, h, w)
+            add_terms(b, h, w)
 
     loop((na - 2) * 2 * CHUNKS, step)
 
@@ -175,8 +187,6 @@
         def _():
             body(b, h)
 
-    loop(na * CHUNKS, lambda i: near(i, lambda b, h: add_terms(b, h, w)))
-    loop(na * CHUNKS, lambda i: near(i, lambda b, h: spread(b, h, w)))
 
     for o in range(1, nw):
         p = lax.rem(w + o, nw)
@@ -189,22 +199,41 @@
         mm(b, h, slot)
         send_terms(b, h, slot)
 
-    loop(na * CHUNKS, lambda i: near(i, each_other(multiply)))
+    def multiply_whole(b):
+        @pl.when((b - a <= na - 2) & (a - b <= na - 2))
+        def _():
+            def one(o):
+                slot = lax.rem(w + 1 + o, nw)
+                mm_whole(b, slot)
+                loop(CHUNKS, lambda h: send_terms(b, h, slot))
+
+            loop(nw - 1, one)
+
+    def late(h):
+        far = na - 1 - a
+        arrive(far, na - 1, jnp.where(a == 0, 1, 0), h)
+        loop(nw, lambda slot: multiply(far, h, slot))
+        loop(nw, lambda slot: add_terms(far, h, slot))
+
+    end = (a == 0) | (a == na - 1)
+    loop(na, multiply_whole)
     loop(na * CHUNKS, lambda i: near(i, each_other(add_terms)))
-    loop(na * CHUNKS, lambda i: near(i, each_other(spread)))
-
-    @pl.when((a == 0) | (a == na - 1))
+    loop(na * CHUNKS, lambda i: near(i, lambda b, h: spread(b, h, w)))
+    pl.when(end)(lambda: loop(CHUNKS - 1, late))
+
+    def prompt(b, h):
+        pl.when((b - a != 1) & (a - b != 1))(lambda: each_other(spread)(b, h))
+
+    def queued(b, h):
+        pl.when((b - a == 1) | (a - b == 1))(lambda: each_other(spread)(b, h))
+
+    loop(na * CHUNKS, lambda i: near(i, prompt))
+    pl.when(end)(lambda: late(CHUNKS - 1))
+    loop(na * CHUNKS, lambda i: near(i, queued))
+
+    @pl.when(end)
     def _():
-        far = na - 1 - a
-        dr = jnp.where(a == 0, 1, 0)
-
-        def last(h):
-            arrive(far, na - 1, dr, h)
-            loop(nw, lambda slot: multiply(far, h, slot))
-            loop(nw, lambda slot: add_terms(far, h, slot))
-            loop(nw, lambda slot: spread(far, h, slot))
-
-        loop(CHUNKS, last)
+        loop(CHUNKS, lambda h: loop(nw, lambda slot: spread(na - 1 - a, h, slot)))
 
     def collect(i):
         b, h = lax.div(i, CHUNKS), lax.rem(i, CHUNKS)
@@ -271,21 +300,24 @@
     kept = hist[...]
     lane = lax.broadcasted_iota(jnp.int32, kept.shape, 1)
     new = jnp.where(lane == 0, best, pltpu.roll(kept, 1, 1))
-    peaks[...] = best
     history[...] = new
-    scales[...] = float_limit / jnp.maximum(jnp.max(new, axis=1, keepdims=True), 1.0)
+    scale = float_limit / jnp.maximum(jnp.max(new, axis=1, keepdims=True), 1.0)
+    for i in range(kept.shape[0]):
+        peaks[i] = best[i, 0]
+        scales[i] = scale[i, 0]
     for o in range(1, n):
         copy(o, o).wait_send()
 
 
 def all_max(values, hist, n):
     vmem = pl.BlockSpec(memory_space=pltpu.VMEM)
-    column = jax.ShapeDtypeStruct((hist.shape[0], 1), jnp.float32)
+    column = jax.ShapeDtypeStruct((hist.shape[0],), jnp.float32)
+    smem = pl.BlockSpec(memory_space=pltpu.SMEM)
     return pl.pallas_call(
         functools.partial(peak_kernel, n),
         out_shape=(column, jax.ShapeDtypeStruct(hist.shape, hist.dtype), column),
         in_specs=[vmem] * 2,
-        out_specs=[vmem] * 3,
+        out_specs=[smem, vmem, smem],
         scratch_shapes=[
             pltpu.VMEM((n,) + values.shape, values.dtype),
             pltpu.SemaphoreType.DMA((n,)),
@@ -302,8 +334,8 @@
             first = (a * sa + w * sw) * cols
             summed[:, first:first + cols] = parts[a, 0, 0, w].astype(jnp.float32)
     x = summed[...]
-    stream = residual[...].astype(jnp.float32) + rms_norm(x, post_gain[...])
-    normed = rms_norm(stream, pre_gain[...])
+    stream = residual[...].astype(jnp.float32) + rms_norm(x, post_gain[...].reshape(1, -1))
+    normed = rms_norm(stream, pre_gain[...].reshape(1, -1))
     s = scale[0]
     cast_out[...] = (jnp.clip(normed * s, -float_limit, float_limit) / s).astype(cast_out.dtype)
     stream_out[...] = stream.astype(stream_out.dtype)
@@ -325,7 +357,7 @@
     na, chunks, nt, nw, rr, cols = parts.shape
     width = residual.shape[1]
     rows = pl.BlockSpec((rr, width), lambda h, k: (h * nt + k, 0))
-    gain = pl.BlockSpec((1, width), lambda h, k: (0, 0))
+    gain = pl.BlockSpec((width,), lambda h, k: (0,))
     kind = jax.ShapeDtypeStruct(residual.shape, jnp.bfloat16)
     return pl.pallas_call(
         functools.partial(finish_kernel, (long, short, cols)),
@@ -338,7 +370,7 @@
         ],
         out_specs=[rows, rows, pl.BlockSpec((8, 128), lambda h, k: (0, 0))],
         scratch_shapes=[pltpu.VMEM((rr, width), jnp.float32)],
-    )(cast_scale, parts, residual, post_gain[None], pre_gain[None])
+    )(cast_scale, parts, residual, post_gain, pre_gain)
 
 
 def project(hidden, down_weight, long, short, nt):
@@ -378,7 +410,7 @@
     parts = project(hidden, down_weight.T, long, short, nt)
     cast_out, stream, tile = finish(parts, residual, post_gain, pre_gain, cast_scale, long, short)
     peaks, new_history, new_scales = all_max(tile, amax_history, long[0] * short[0])
-    return (cast_out, stream, peaks[:, 0], new_history, new_scales[:, 0])
+    return (cast_out, stream, peaks, new_history, new_scales)
 
 
 def solution(mesh):

time: 245 us -> 213 us (0.87)
  Pallas kernels: 237 us -> 207 us
  other arithmetic: 2.58 us -> 0 us
    pallas_call x1, Pallas kernels: 219 us -> 190 us  [project(): pl.pallas_call(functools.partial(project_kernel, (long, short, nt, half,...]
    broadcast_in_dim x2 -> x0, local copies, waits for them, and re-layouts: 2.68 us -> none  [the longest x1 1.34 us: finish(): post_gain[None]]
    pallas_call x2 -> x0, other arithmetic: 2.58 us -> none  [all_max(): pl.pallas_call(functools.partial(peak_kernel, n), out_shape=(column, jax....]
where the time goes in v3:
time: 213 us; the launch traced here: 212 us
  Pallas kernels  207 us (97%)
  local copies, waits for them, and re-layouts  3.65 us (2%)
    pallas_call x1, Pallas kernels, project(): pl.pallas_call(functools.partial(project_kernel, (long, short, nt, half,...  190 us
    pallas_call x1, Pallas kernels, finish(): pl.pallas_call(functools.partial(finish_kernel, (long, short, cols)), gri...  9.35 us
    pallas_call x1, Pallas kernels, all_max(): pl.pallas_call(functools.partial(peak_kernel, n), out_shape=(column, jax....  8.07 us

profile of v3, /device:TPU:0, one launch (start us, length us, event | category | flops | bytes accessed | tf_op | source)
XLA Modules:
  0.0 212.4 jit_solution(14189532537213460819)
XLA Ops:
  1.3 190.0 %shard_map.110.parts = bf16[4,2,4,2,32,576]{5,4,3,2,1,0:T(8,128)(2,1)} custom-call(bf16[256,4608]{1,0:T(8,128)(2,1)} %hid.1, bf16[576,4608]{1,0:T(8,128)(2,1)} %bitcast.1), custom_call_target="tpu_custom_call" | custom-call | tf_op jit(solution)/shard_map/pallas_call | solution.py:384
  191.3 9.4 %shard_map.111 = (bf16[256,4608]{1,0:T(8,128)(2,1)}, bf16[256,4608]{1,0:T(8,128)(2,1)}, f32[8,128]{1,0:T(8,128)}) custom-call(f32[1]{0:T(128)S(6)} %copy.15.scale, bf16[4,2,4,2,32,576]{5,4,3,2,1,0:T(8,128)(2,1)} %shard_map.110.parts, bf16[256,4608]{1,0:T(8,128)(2,1)} %residual.1, f32[4608]{0:T(1024)} %post_gain.1, f32[4608]{0:T(1024)} %pre_gain.1), custom_call_target="tpu_custom_call" | custom-call | tf_op jit(solution)/shard_map/pallas_call | solution.py:362
  200.6 8.1 %shard_map.112 = (f32[3]{0:T(128)}, f32[3,1024]{1,0:T(4,128)}, f32[3]{0:T(128)}) custom-call(f32[8,128]{1,0:T(8,128)} %get-tuple-element.13.x, f32[3,1024]{1,0:T(4,128)} %hist.1), custom_call_target="tpu_custom_call" | custom-call | tf_op jit(solution)/shard_map/pallas_call | solution.py:316
  208.7 1.2 copy.16
  209.9 1.3 copy.17
  211.2 1.1 copy.18

commit v4 on v3

--- a/solution.py
+++ b/solution.py
@@ -227,13 +227,18 @@
     def queued(b, h):
         pl.when((b - a == 1) | (a - b == 1))(lambda: each_other(spread)(b, h))
 
+    def far_spread(h):
+        loop(nw, lambda slot: spread(na - 1 - a, h, slot))
+
     loop(na * CHUNKS, lambda i: near(i, prompt))
-    pl.when(end)(lambda: late(CHUNKS - 1))
-    loop(na * CHUNKS, lambda i: near(i, queued))
 
     @pl.when(end)
     def _():
-        loop(CHUNKS, lambda h: loop(nw, lambda slot: spread(na - 1 - a, h, slot)))
+        loop(CHUNKS - 1, far_spread)
+        late(CHUNKS - 1)
+
+    loop(na * CHUNKS, lambda i: near(i, queued))
+    pl.when(end)(lambda: far_spread(CHUNKS - 1))
 
     def collect(i):
         b, h = lax.div(i, CHUNKS), lax.rem(i, CHUNKS)
@@ -277,7 +282,7 @@
         copy(wei, wbuf.at[w], w_send.at[p], w_recv.at[w], dev(a, p, t)).wait_send()
 
 
-def peak_kernel(n, x, hist, peaks, history, scales, got, ss, rs):
+def peak_kernel(n, x, out, got, ss, rs):
     d = lax.axis_index("dp")
     t = lax.axis_index("tensor")
     barrier = pltpu.get_barrier_semaphore()
@@ -296,8 +301,14 @@
     for o in range(1, n):
         copy(o, o).wait_recv()
         best = jnp.maximum(best, got[o])
-    best = best[:3, :1]
+    out[...] = best
+    for o in range(1, n):
+        copy(o, o).wait_send()
+
+
+def history_kernel(x, hist, peaks, history, scales):
     kept = hist[...]
+    best = x[:kept.shape[0], :1]
     lane = lax.broadcasted_iota(jnp.int32, kept.shape, 1)
     new = jnp.where(lane == 0, best, pltpu.roll(kept, 1, 1))
     history[...] = new
@@ -305,26 +316,30 @@
     for i in range(kept.shape[0]):
         peaks[i] = best[i, 0]
         scales[i] = scale[i, 0]
-    for o in range(1, n):
-        copy(o, o).wait_send()
 
 
 def all_max(values, hist, n):
     vmem = pl.BlockSpec(memory_space=pltpu.VMEM)
-    column = jax.ShapeDtypeStruct((hist.shape[0],), jnp.float32)
     smem = pl.BlockSpec(memory_space=pltpu.SMEM)
-    return pl.pallas_call(
+    best = pl.pallas_call(
         functools.partial(peak_kernel, n),
-        out_shape=(column, jax.ShapeDtypeStruct(hist.shape, hist.dtype), column),
-        in_specs=[vmem] * 2,
-        out_specs=[smem, vmem, smem],
+        out_shape=jax.ShapeDtypeStruct(values.shape, values.dtype),
+        in_specs=[vmem],
+        out_specs=vmem,
         scratch_shapes=[
             pltpu.VMEM((n,) + values.shape, values.dtype),
             pltpu.SemaphoreType.DMA((n,)),
             pltpu.SemaphoreType.DMA((n,)),
         ],
         compiler_params=pltpu.CompilerParams(collective_id=1, has_side_effects=True),
-    )(values, hist)
+    )(values)
+    column = jax.ShapeDtypeStruct((hist.shape[0],), jnp.float32)
+    return pl.pallas_call(
+        history_kernel,
+        out_shape=(column, jax.ShapeDtypeStruct(hist.shape, hist.dtype), column),
+        in_specs=[vmem] * 2,
+        out_specs=[smem, vmem, smem],
+    )(best, hist)
 
 
 def finish_kernel(dims, scale, parts, residual, post_gain, pre_gain, cast_out, stream_out, peaks, summed):

time: 213 us -> 207 us (0.972)
  local copies, waits for them, and re-layouts: 3.65 us -> 0 us
    unnamed x3 -> x0, local copies, waits for them, and re-layouts: 3.65 us -> none
    pallas_call x1, Pallas kernels: 190 us -> 186 us  [project(): pl.pallas_call(functools.partial(project_kernel, (long, short, nt, half,...]
    pallas_call x1 -> x2, Pallas kernels: 8.07 us -> 9.27 us  [the longest x1 7.82 us: all_max(): pl.pallas_call(functools.partial(peak_kernel, n), out_shape=jax.ShapeDtyp...]
where the time goes in v4:
time: 207 us; the launch traced here: 206 us
  Pallas kernels  205 us (99%)
    pallas_call x1, Pallas kernels, project(): pl.pallas_call(functools.partial(project_kernel, (long, short, nt, half,...  186 us
    pallas_call x1, Pallas kernels, finish(): pl.pallas_call(functools.partial(finish_kernel, (long, short, cols)), gri...  9.35 us
    pallas_call x1, Pallas kernels, all_max(): pl.pallas_call(functools.partial(peak_kernel, n), out_shape=jax.ShapeDtyp...  7.82 us

profile of v4, /device:TPU:0, one launch (start us, length us, event | category | flops | bytes accessed | tf_op | source)
XLA Modules:
  0.0 206.4 jit_solution(15504107401591940143)
XLA Ops:
  1.3 186.5 %shard_map.110.parts = bf16[4,2,4,2,32,576]{5,4,3,2,1,0:T(8,128)(2,1)} custom-call(bf16[256,4608]{1,0:T(8,128)(2,1)} %hid.1, bf16[576,4608]{1,0:T(8,128)(2,1)} %bitcast.1), custom_call_target="tpu_custom_call" | custom-call | tf_op jit(solution)/shard_map/pallas_call | solution.py:399
  187.8 9.4 %shard_map.111 = (bf16[256,4608]{1,0:T(8,128)(2,1)}, bf16[256,4608]{1,0:T(8,128)(2,1)}, f32[8,128]{1,0:T(8,128)}) custom-call(f32[1]{0:T(128)S(6)} %copy.12.scale, bf16[4,2,4,2,32,576]{5,4,3,2,1,0:T(8,128)(2,1)} %shard_map.110.parts, bf16[256,4608]{1,0:T(8,128)(2,1)} %residual.1, f32[4608]{0:T(1024)} %post_gain.1, f32[4608]{0:T(1024)} %pre_gain.1), custom_call_target="tpu_custom_call" | custom-call | tf_op jit(solution)/shard_map/pallas_call | solution.py:377
  197.1 7.8 %shard_map.112.x = f32[8,128]{1,0:T(8,128)} custom-call(f32[8,128]{1,0:T(8,128)} %get-tuple-element.13.x), custom_call_target="tpu_custom_call" | custom-call | tf_op jit(solution)/shard_map/pallas_call | solution.py:324
  204.9 1.4 shard_map.113

commit v5 on v4

--- a/solution.py
+++ b/solution.py
@@ -342,7 +342,7 @@
     )(best, hist)
 
 
-def finish_kernel(dims, scale, parts, residual, post_gain, pre_gain, cast_out, stream_out, peaks, summed):
+def finish_kernel(dims, scale, parts, residual, post_gain, pre_gain, cast_out, stream_out, peaks, summed, tops):
     (na, sa), (nw, sw), cols = dims
     for a in range(na):
         for w in range(nw):
@@ -352,20 +352,26 @@
     stream = residual[...].astype(jnp.float32) + rms_norm(x, post_gain[...].reshape(1, -1))
     normed = rms_norm(stream, pre_gain[...].reshape(1, -1))
     s = scale[0]
-    cast_out[...] = (jnp.clip(normed * s, -float_limit, float_limit) / s).astype(cast_out.dtype)
+    inverse = 1.0 / jnp.full((1, 1), s, jnp.float32)
+    cast_out[...] = (jnp.clip(normed * s, -float_limit, float_limit) * inverse).astype(cast_out.dtype)
     stream_out[...] = stream.astype(stream_out.dtype)
-    row = lax.broadcasted_iota(jnp.int32, peaks.shape, 0)
-    tops = [jnp.max(jnp.abs(v)) for v in (x, stream, normed)]
-    tile = jnp.where(row == 0, tops[0], jnp.where(row == 1, tops[1], tops[2]))
     first_step = (pl.program_id(0) == 0) & (pl.program_id(1) == 0)
+    last_step = (pl.program_id(0) == pl.num_programs(0) - 1) & (
+        pl.program_id(1) == pl.num_programs(1) - 1)
 
     @pl.when(first_step)
     def _():
-        peaks[...] = tile
-
-    @pl.when(jnp.logical_not(first_step))
+        tops[...] = jnp.zeros_like(tops)
+
+    for i, v in enumerate((x, stream, normed)):
+        most = jnp.max(jnp.abs(v).reshape(-1, 8, v.shape[1]), axis=0)
+        tops[i] = jnp.maximum(tops[i], most)
+
+    @pl.when(last_step)
     def _():
-        peaks[...] = jnp.maximum(peaks[...], tile)
+        row = lax.broadcasted_iota(jnp.int32, peaks.shape, 0)
+        best = [jnp.max(tops[i]) for i in range(3)]
+        peaks[...] = jnp.where(row == 0, best[0], jnp.where(row == 1, best[1], best[2]))
 
 
 def finish(parts, residual, post_gain, pre_gain, cast_scale, long, short):
@@ -384,7 +390,10 @@
             rows, gain, gain,
         ],
         out_specs=[rows, rows, pl.BlockSpec((8, 128), lambda h, k: (0, 0))],
-        scratch_shapes=[pltpu.VMEM((rr, width), jnp.float32)],
+        scratch_shapes=[
+            pltpu.VMEM((rr, width), jnp.float32),
+            pltpu.VMEM((3, 8, width), jnp.float32),
+        ],
     )(cast_scale, parts, residual, post_gain, pre_gain)
 
 

time: 207 us -> 207 us (level)
  no operation moved by 1% of the time
where the time goes in v5:
time: 207 us; the launch traced here: 206 us
  Pallas kernels  205 us (99%)
    pallas_call x1, Pallas kernels, project(): pl.pallas_call(functools.partial(project_kernel, (long, short, nt, half,...  186 us
    pallas_call x1, Pallas kernels, finish(): pl.pallas_call(functools.partial(finish_kernel, (long, short, cols)), gri...  9.41 us
    pallas_call x1, Pallas kernels, all_max(): pl.pallas_call(functools.partial(peak_kernel, n), out_shape=jax.ShapeDtyp...  7.82 us

profile of v5, /device:TPU:0, one launch (start us, length us, event | category | flops | bytes accessed | tf_op | source)
XLA Modules:
  0.0 206.4 jit_solution(7628762646465075034)
XLA Ops:
  1.3 186.5 %shard_map.110.parts = bf16[4,2,4,2,32,576]{5,4,3,2,1,0:T(8,128)(2,1)} custom-call(bf16[256,4608]{1,0:T(8,128)(2,1)} %hid.1, bf16[576,4608]{1,0:T(8,128)(2,1)} %bitcast.1), custom_call_target="tpu_custom_call" | custom-call | tf_op jit(solution)/shard_map/pallas_call | solution.py:408
  187.8 9.4 %shard_map.111 = (bf16[256,4608]{1,0:T(8,128)(2,1)}, bf16[256,4608]{1,0:T(8,128)(2,1)}, f32[8,128]{1,0:T(8,128)}) custom-call(f32[1]{0:T(128)S(6)} %copy.12.scale, bf16[4,2,4,2,32,576]{5,4,3,2,1,0:T(8,128)(2,1)} %shard_map.110.parts, bf16[256,4608]{1,0:T(8,128)(2,1)} %residual.1, f32[4608]{0:T(1024)} %post_gain.1, f32[4608]{0:T(1024)} %pre_gain.1), custom_call_target="tpu_custom_call" | custom-call | tf_op jit(solution)/shard_map/pallas_call | solution.py:383
  197.2 7.8 %shard_map.112.x = f32[8,128]{1,0:T(8,128)} custom-call(f32[8,128]{1,0:T(8,128)} %get-tuple-element.13.x), custom_call_target="tpu_custom_call" | custom-call | tf_op jit(solution)/shard_map/pallas_call | solution.py:324
  205.0 1.4 shard_map.113
